TPU v7x, 128 devices: a whole 4x4x4 slice. The times are simulated.
128 devices in a mesh: dp: 8 (over x, core), mp: 16 (over y, z).
Axes of the slice: x: 4, y: 4, z: 4, core: 2. Of those that a mesh axis runs over, the one named last changes fastest.
Arguments:
- tokens: bfloat16 [256, 8192], P('dp', 'mp'), may hold values from -6 to 6
- gate_up_weight: bfloat16 [2, 8192, 15360], P(None, 'mp', 'dp'), may hold values from -0.0625 to 0.0625
- down_weight: bfloat16 [15360, 8192], P('dp', 'mp'), may hold values from -0.046875 to 0.046875
- gate_up_input_factor: bfloat16 [2, 8192, 64], P(None, 'mp'), may hold values from -0.0625 to 0.0625
- gate_up_output_factor: bfloat16 [2, 64, 15360], P(None, None, 'dp'), may hold values from -0.046875 to 0.046875
- down_input_factor: bfloat16 [15360, 64], P('dp'), may hold values from -0.046875 to 0.046875
- down_output_factor: bfloat16 [64, 8192], P(None, 'mp'), may hold values from -0.0625 to 0.0625
- cotangent: bfloat16 [256, 8192], P('dp', 'mp'), may hold values from -6 to 6
Outputs:
- output: bfloat16 [256, 8192], P('dp', 'mp')
- input_grad: bfloat16 [256, 8192], P('dp', 'mp')
- grad_gate_up_lower: float32 [2, 8192, 64], P(None, 'mp')
- gate_up_output_factor_gradient: float32 [2, 64, 15360], P(None, None, 'dp')
- down_input_factor_gradient: float32 [15360, 64], P('dp')
- down_output_factor_gradient: float32 [64, 8192], P(None, 'mp')
All inputs are finite; a program needn't handle non-finite values.
Results may differ from a plain program's by a relative error of at most 0.0065.
Values may be sent and summed in bfloat16 or wider, within the bound.
A program may use at most 64 MiB of HBM per device.

v0:
```python
import jax
import jax.numpy as jnp
from jax import lax
from jax.sharding import Mesh
from jax.sharding import PartitionSpec as P

MP = ("mp_0", "mp_1")
adapter_scale = 2.0


def sent_to_all(array, axis):
    length = lax.axis_size(axis)
    return lax.all_to_all(
        jnp.broadcast_to(array[None], (length, *array.shape)), axis, 0, 0, tiled=True
    )


def joined_along(parts, dim):
    shape = list(parts.shape[1:])
    shape[dim] *= parts.shape[0]
    return jnp.moveaxis(parts, 0, dim).reshape(shape)


def gathered_copies(array, axis, dim):
    parts = sent_to_all(array, axis)
    return joined_along(parts, dim)


def cut_along(array, dim, length):
    shape = array.shape
    parts = array.reshape(*shape[:dim], length, shape[dim] // length, *shape[dim + 1 :])
    return jnp.moveaxis(parts, dim, 0)


def piece_ends(length, count):
    hop = length // count
    if hop >= 8:
        hop -= hop % 8
    return [hop * k for k in range(1, count)]


def sum_in_order(parts, axes, turns):
    shape = [lax.axis_size(a) for a in axes]
    parts = parts.reshape(*shape, *parts.shape[1:])
    parts = parts.transpose(*turns, *range(len(axes), parts.ndim))
    parts = parts.reshape(-1, *parts.shape[len(axes) :])
    for k in turns:
        parts = lax.psum_scatter(parts, axes[k], scatter_dimension=0, tiled=True)
    return parts[0]


def sum_at_once(array, axes, dim):
    parts = cut_along(array, dim, lax.axis_size(axes))
    widest = max(range(1, max(2, parts.ndim - 1)), key=lambda d: parts.shape[d])
    count, finished = (len(axes), [])
    for first, section in enumerate(
        jnp.split(parts, piece_ends(parts.shape[widest], count), axis=widest)
    ):
        if section.size:
            turns = [(first + k) % count for k in range(count)]
            finished.append(sum_in_order(section, axes, turns))
    return jnp.concatenate(finished, axis=widest - 1)


def sum_at_owner(array, axis, dim):
    parts = cut_along(array, dim, lax.axis_size(axis))
    arrived = lax.all_to_all(parts, axis, split_axis=0, concat_axis=0, tiled=True)
    return arrived.sum(axis=0)


def over_copies(array, axis):
    return sent_to_all(array, axis).sum(axis=0)


def in_one(arrays, axis):
    ravelled, at, finished = (jnp.concatenate([a.reshape(-1) for a in arrays]), 0, [])
    so_far = over_copies(ravelled, axis)
    for a in arrays:
        finished.append(so_far[at : at + a.size].reshape(a.shape))
        at += a.size
    return tuple(finished)


def contract_trailing(left, right, matmul_precision=None):
    return lax.dot_general(
        left,
        right,
        (((1,), (1,)), ((), ())),
        preferred_element_type=jnp.float32,
        precision=matmul_precision,
    )


def contract_leading(left, right, matmul_precision=None):
    return lax.dot_general(
        left,
        right,
        (((0,), (0,)), ((), ())),
        preferred_element_type=jnp.float32,
        precision=matmul_precision,
    )


def per_device(
    tokens,
    gate_up_weight,
    down_weight,
    gate_up_input_factor,
    gate_up_output_factor,
    down_input_factor,
    down_output_factor,
    cotangent,
):
    single_float = jnp.float32
    product_precision = lax.Precision.DEFAULT
    tok_rows = tokens.shape[0]
    input_rows_full = gathered_copies(tokens, "dp", 0)
    total = input_rows_full.shape[0]
    mp_rows = total // lax.axis_size(MP)
    scale_factor = total ** (-0.5)
    mp_start = lax.axis_index(MP) * mp_rows
    dp_start = lax.axis_index("dp") * tok_rows
    low_part = jnp.einsum(
        "td,kdr->tkr", input_rows_full, gate_up_input_factor, preferred_element_type=single_float
    )
    upper_widened = gate_up_output_factor.astype(single_float)
    term = jnp.einsum(
        "td,kdf->tkf", input_rows_full, gate_up_weight, preferred_element_type=single_float
    )
    low_slab = low_part
    term = term + adapter_scale * jnp.einsum("ubw,bwa->uba", low_slab, upper_widened)
    preactivation = sum_at_once(term, MP, 0)
    gate = preactivation[:, 0]
    upper = preactivation[:, 1]
    hidden_state = (jax.nn.silu(gate) * upper).astype(jnp.bfloat16)
    hidden_state_full = gathered_copies(hidden_state, MP, 0)
    low_down_part = jnp.dot(
        hidden_state_full, down_input_factor, preferred_element_type=single_float
    )
    down_widened_rows = down_output_factor.astype(single_float)
    term = jnp.dot(hidden_state_full, down_weight, preferred_element_type=single_float)
    low_slab = low_down_part
    term = term + adapter_scale * jnp.dot(low_slab, down_widened_rows)
    output = sum_at_owner(term, "dp", 0)
    output = output.astype(jnp.bfloat16)
    cot_all = gathered_copies(cotangent, "dp", 0)
    coeff_part = contract_leading(
        low_down_part, cot_all.astype(single_float), matmul_precision=product_precision
    )
    backward_down_rows = over_copies(contract_trailing(cot_all, down_output_factor), MP).astype(
        jnp.bfloat16
    )
    hidden_state_gradient = lax.psum_scatter(
        contract_trailing(cot_all, down_weight), MP, scatter_dimension=0, tiled=True
    )
    backward_row_block = lax.dynamic_slice_in_dim(backward_down_rows, mp_start, mp_rows, 0)
    hidden_state_gradient = hidden_state_gradient + adapter_scale * contract_trailing(
        backward_row_block, down_input_factor
    )
    down_input_factor_gradient = (
        adapter_scale * scale_factor * contract_leading(hidden_state_full, backward_down_rows)
    )
    sigma = jax.nn.sigmoid(gate)
    gate_back = hidden_state_gradient * upper * sigma * (1.0 + gate * (1.0 - sigma))
    up_back = hidden_state_gradient * gate * sigma
    pre_back = jnp.stack([gate_back, up_back], axis=1).astype(jnp.bfloat16)
    back_all = gathered_copies(pre_back, MP, 0)
    upper_partial = jnp.einsum("tkr,tkf->krf", low_part, back_all.astype(single_float))
    gate_up_output_factor_gradient = adapter_scale * scale_factor * lax.psum(upper_partial, MP)
    back_low_part = jnp.einsum(
        "tkf,krf->tkr", back_all, gate_up_output_factor, preferred_element_type=single_float
    )
    back_low_sum, down_coefficient = in_one((back_low_part, coeff_part), "dp")
    down_output_factor_gradient = adapter_scale * scale_factor * down_coefficient
    backward_lower_rows = back_low_sum.astype(jnp.bfloat16)
    grad_gate_up_lower = (
        adapter_scale
        * scale_factor
        * jnp.einsum(
            "qi,qps->pis", input_rows_full, backward_lower_rows, preferred_element_type=single_float
        )
    )
    input_total_sum = sum_at_owner(
        jnp.einsum("tkf,kdf->td", back_all, gate_up_weight, preferred_element_type=single_float),
        "dp",
        0,
    )
    low_rows_back = lax.dynamic_slice_in_dim(backward_lower_rows, dp_start, tok_rows, 0)
    input_total_sum = input_total_sum + adapter_scale * jnp.einsum(
        "tkr,kdr->td", low_rows_back, gate_up_input_factor, preferred_element_type=single_float
    )
    input_grad = input_total_sum.astype(jnp.bfloat16)
    return (
        output,
        input_grad,
        grad_gate_up_lower,
        gate_up_output_factor_gradient,
        down_input_factor_gradient,
        down_output_factor_gradient,
    )


def solution(mesh):
    torus = Mesh(mesh.devices.reshape(mesh.shape["dp"], 4, 4), ("dp", "mp_0", "mp_1"))
    in_specs = (
        P("dp", MP),
        P(None, MP, "dp"),
        P("dp", MP),
        P(None, MP, None),
        P(None, None, "dp"),
        P("dp", None),
        P(None, MP),
        P("dp", MP),
    )
    out_specs = (
        P("dp", MP),
        P("dp", MP),
        P(None, MP, None),
        P(None, None, "dp"),
        P("dp", None),
        P(None, MP),
    )
    return jax.shard_map(
        per_device, mesh=torus, in_specs=in_specs, out_specs=out_specs, check_vma=False
    )
```

profile of v0, /device:TPU:0, one launch (start us, length us, event | category | flops | bytes accessed | tf_op | source)
XLA Modules:
  0.0 345.4 jit_solution(7605972328173418897)
XLA Ops:
  8.0 0.0 reduce-scatter.9.cloned.1.call-start
  8.1 0.9 broadcast_in_dim.12
  9.0 11.7 %all_to_all.41 = bf16[8,32,512]{2,1,0:T(8,128)(2,1)S(1)} all-to-all(bf16[8,32,512]{2,1,0:T(8,128)(2,1)S(1)} %broadcast_in_dim.12), channel_id=1, replica_groups=mesh['dp'=8,'mp_0'=4,'mp_1'=4] {'dp'}, dimensions={0} | all-to-all | bytes 524288 | tf_op jit(solution)/shard_map/all_to_all | solution.py:13
  20.7 3.4 fusion.22
  24.1 0.2 fusion.23
  24.3 0.7 bitcast_add_fusion
  25.0 1.6 fusion.19
  26.6 1.4 copy.44
  28.0 0.0 reduce-scatter.9.cloned.1.call-update
  28.0 0.0 reduce-scatter.5.cloned.1.call-start
  28.1 3.0 copy.52
  31.1 0.0 all-reduce.6.cloned.1.call-start
  31.1 0.7 copy-done.12
  31.8 9.9 %all_to_all.42 = bf16[8,32,512]{2,1,0:T(8,128)(2,1)S(1)} all-to-all(bf16[8,32,512]{2,1,0:T(8,128)(2,1)S(1)} %broadcast_in_dim.14), channel_id=1, replica_groups=mesh['dp'=8,'mp_0'=4,'mp_1'=4] {'dp'}, dimensions={0} | all-to-all | bytes 524288 | tf_op jit(solution)/shard_map/all_to_all | solution.py:13
  41.8 2.0 fusion.25
  43.8 0.0 all-reduce.6.cloned.1.call-update
  43.8 0.0 reduce-scatter.11.cloned.1.call-start
  43.8 14.1 %reduce-scatter.9.cloned.1.call-done = f32[4,8,2,1920]{3,1,2,0:T(8,128)} async-done(((f32[16,8,2,1920]{3,1,2,0:T(8,128)}), f32[4,8,2,1920]{3,1,2,0:T(8,128)}) %reduce-scatter.9.cloned.1.call-update) | async-done | bytes 491536 | tf_op jit(solution)/shard_map/reduce_scatter | solution.py:48
  58.0 0.2 fusion.26
  58.2 1.1 broadcast_in_dim.15
  59.3 5.5 %all-to-all-start.4 = ((f32[16,256,64]{1,2,0:T(8,128)}), f32[16,256,64]{1,2,0:T(8,128)}, u32[]{:S(2)}, u32[]{:S(2)}) async-start(f32[16,256,64]{1,2,0:T(8,128)} %broadcast_in_dim.15), calls=%async_computation.8 | async-start | bytes 2097152 | tf_op jit(solution)/shard_map/all_to_all | solution.py:13
  64.7 0.0 reduce-scatter.7.cloned.1.call-start
  64.8 32.6 %reduce-scatter.5.cloned.1.call-done = f32[4,8,2,1920]{3,1,2,0:T(8,128)} async-done(((f32[16,8,2,1920]{3,1,2,0:T(8,128)}), f32[4,8,2,1920]{3,1,2,0:T(8,128)}) %reduce-scatter.5.cloned.1.call-update) | async-done | bytes 491536 | tf_op jit(solution)/shard_map/reduce_scatter | solution.py:48
  97.4 0.6 dynamic-slice
  98.6 1.3 reduce_sum.37
  99.9 46.6 %all-reduce.6.cloned.1.call-done = f32[256,1920]{1,0:T(8,128)} async-done(((f32[256,1920]{1,0:T(8,128)}), f32[256,1920]{1,0:T(8,128)}) %all-reduce.6.cloned.1.call-update) | async-done | bytes 1966096
  146.5 2.1 fusion.15
  148.6 1.0 broadcast_in_dim.13
  149.6 4.9 %all-to-all-start.1 = ((bf16[16,16,1920]{2,1,0:T(8,128)(2,1)}), bf16[16,16,1920]{2,1,0:T(8,128)(2,1)S(1)}, u32[]{:S(2)}, u32[]{:S(2)}) async-start(bf16[16,16,1920]{2,1,0:T(8,128)(2,1)} %broadcast_in_dim.13), calls=%async_computation.5 | async-start | bytes 1966080 | tf_op jit(solution)/shard_map/all_to_all | solution.py:13
  154.6 1.5 pad_maximum_fusion.2
  156.1 14.7 %all-to-all-done.1 = bf16[16,16,1920]{2,1,0:T(8,128)(2,1)S(1)} async-done(((bf16[16,16,1920]{2,1,0:T(8,128)(2,1)}), bf16[16,16,1920]{2,1,0:T(8,128)(2,1)S(1)}, u32[]{:S(2)}, u32[]{:S(2)}) %all-to-all-start.1) | async-done | bytes 983072 | tf_op jit(solution)/shard_map/all_to_all | solution.py:13
  170.8 2.3 broadcast_in_dim.16
  173.1 4.4 %all-to-all-start.5 = ((bf16[16,16,2,1920]{3,1,2,0:T(8,128)(2,1)}), bf16[16,16,2,1920]{3,1,2,0:T(8,128)(2,1)}, u32[]{:S(2)}, u32[]{:S(2)}) async-start(bf16[16,16,2,1920]{3,1,2,0:T(8,128)(2,1)} %broadcast_in_dim.16), calls=%async_computation.9 | async-start | bytes 3932160 | tf_op jit(solution)/shard_map/all_to_all | solution.py:13
  177.5 1.4 fusion.24
  178.9 0.2 convolution_bitcast_fusion.1
  179.0 0.7 copy.54
  179.7 0.2 convolution_multiply_fusion.2
  180.0 1.5 convolution_add_fusion
  181.5 22.5 %all-to-all-done.5 = bf16[16,16,2,1920]{3,1,2,0:T(8,128)(2,1)} async-done(((bf16[16,16,2,1920]{3,1,2,0:T(8,128)(2,1)}), bf16[16,16,2,1920]{3,1,2,0:T(8,128)(2,1)}, u32[]{:S(2)}, u32[]{:S(2)}) %all-to-all-start.5) | async-done | bytes 1966112 | tf_op jit(solution)/shard_map/all_to_all | solution.py:13
  204.0 4.3 %all-to-all-start.2 = ((f32[8,32,512]{2,1,0:T(8,128)}), f32[8,32,512]{2,1,0:T(8,128)}, u32[]{:S(2)}, u32[]{:S(2)}) async-start(f32[8,32,512]{2,1,0:T(8,128)} %bitcast.110), calls=%async_computation.6 | async-start | bytes 1048576 | tf_op jit(solution)/shard_map/all_to_all | solution.py:67
  208.2 1.7 copy.45
  210.0 1.3 copy-done.1
  211.3 1.4 convolution_bitcast_fusion
  212.7 1.0 copy.46
  213.7 0.8 reshape.119
  214.5 4.7 %fusion.3 = f32[8,32,512]{2,1,0:T(8,128)} fusion(bf16[8,32,1920,2]{2,1,0,3:T(8,128)(2,1)} %bitcast.96, bf16[2,512,1920]{2,1,0:T(8,128)(2,1)} %param.9), kind=kOutput, calls=%fused_computation.6 | convolution fusion | flops 1006632960 | bytes 6422528 | tf_op jit(solution)/shard_map/tkf,kdf->td/dot_general | solution.py:184
  219.3 4.8 %all-to-all-start.6 = ((f32[8,32,512]{2,1,0:T(8,128)}), f32[8,32,512]{2,1,0:T(8,128)}, u32[]{:S(2)}, u32[]{:S(2)}) async-start(f32[8,32,512]{2,1,0:T(8,128)} %fusion.3), calls=%async_computation.10 | async-start | bytes 1048576 | tf_op jit(solution)/shard_map/all_to_all | solution.py:67
  224.1 1.0 pad_maximum_fusion
  225.0 9.4 %all-to-all-done.6 = f32[8,32,512]{2,1,0:T(8,128)} async-done(((f32[8,32,512]{2,1,0:T(8,128)}), f32[8,32,512]{2,1,0:T(8,128)}, u32[]{:S(2)}, u32[]{:S(2)}) %all-to-all-start.6) | async-done | bytes 524320 | tf_op jit(solution)/shard_map/all_to_all | solution.py:67
  234.5 2.4 broadcast_in_dim.17
  236.9 4.5 %all-to-all-start.7 = ((f32[8,1,65536]{2,1,0:T(1,128)}), f32[8,1,65536]{2,1,0:T(1,128)}, u32[]{:S(2)}, u32[]{:S(2)}) async-start(f32[8,1,65536]{2,1,0:T(1,128)} %broadcast_in_dim.17), calls=%async_computation.11 | async-start | bytes 4194304 | tf_op jit(solution)/shard_map/all_to_all | solution.py:13
  241.4 0.2 all-reduce.4.cloned.1.call-start
  241.6 2.9 fusion.27
  244.5 0.0 all-reduce.4.cloned.1.call-update
  244.6 1.1 convolution_multiply_fusion
  245.7 1.7 reduce_sum.36
  247.4 1.1 reduce_sum.38
  248.4 81.9 %all-reduce.4.cloned.1.call-done = f32[2,64,1920]{2,1,0:T(8,128)} async-done(((f32[2,64,1920]{2,1,0:T(8,128)}), f32[2,64,1920]{2,1,0:T(8,128)}) %all-reduce.4.cloned.1.call-update) | async-done | bytes 983056 | tf_op jit(solution)/shard_map/psum | solution.py:169
  330.3 2.2 broadcast_multiply_fusion
  332.5 3.2 reduce_sum.39
  335.7 0.1 convert_element_type.32
  335.8 0.9 fusion.6
  336.8 0.7 mul.128
  337.4 0.8 fusion.9
  (38 shorter events, 0.2 us)
Async XLA Ops:
  8.0 33.8 %copy-start = (bf16[1920,512]{1,0:T(8,128)(2,1)S(1)}, bf16[1920,512]{1,0:T(8,128)(2,1)}, u32[]{:S(2)}) copy-start(bf16[1920,512]{1,0:T(8,128)(2,1)} %param.10) | copy-start | bytes 5898244
  8.0 49.9 %reduce-scatter.9.cloned.1.call-start = ((), (), s32[]{:S(2)}) async-start(), calls=%async_computation.14 | async-start | bytes 2457600 | tf_op jit(solution)/shard_map/reduce_scatter | solution.py:48
  20.7 3.4 copy-start.6
  20.7 3.6 %copy-start.2 = (bf16[2,64,1920]{2,1,0:T(8,128)(2,1)S(1)}, bf16[2,64,1920]{2,1,0:T(8,128)(2,1)}, u32[]{:S(2)}) copy-start(bf16[2,64,1920]{2,1,0:T(8,128)(2,1)} %param.12) | copy-start | bytes 1474564
  24.3 0.7 copy-start.4
  28.0 69.3 %reduce-scatter.5.cloned.1.call-start = ((), (), s32[]{:S(2)}) async-start(), calls=%async_computation.12 | async-start | bytes 2457600 | tf_op jit(solution)/shard_map/reduce_scatter | solution.py:48
  31.1 0.8 copy-start.12
  31.1 115.4 %all-reduce.6.cloned.1.call-start = ((), (), s32[]{:S(2)}) async-start(), calls=%async_computation.17 | async-start | bytes 3932160
  43.8 14.2 %copy-start.8 = (bf16[64,512]{1,0:T(8,128)(2,1)S(1)}, bf16[64,512]{1,0:T(8,128)(2,1)}, u32[]{:S(2)}) copy-start(bf16[64,512]{1,0:T(8,128)(2,1)} %param.14) | copy-start | bytes 196612
  43.8 102.7 %reduce-scatter.11.cloned.1.call-start = ((), (), s32[]{:S(2)}) async-start(), calls=%async_computation.15 | async-start | bytes 614400 | tf_op jit(solution)/shard_map/reduce_scatter | solution.py:48
  58.2 39.2 %copy-start.13 = (u32[128]{0:T(128)S(1)}, u32[128]{0:T(128)}, u32[]{:S(2)}) copy-start(u32[128]{0:T(128)} %constant.41) | copy-start | bytes 1540
  59.2 87.3 %copy-start.9 = (bf16[1920,64]{0,1:T(8,128)(2,1)S(1)}, bf16[1920,64]{0,1:T(8,128)(2,1)}, u32[]{:S(2)}) copy-start(bf16[1920,64]{0,1:T(8,128)(2,1)} %param.13) | copy-start | bytes 737284
  59.3 39.4 %all-to-all-start.4 = ((f32[16,256,64]{1,2,0:T(8,128)}), f32[16,256,64]{1,2,0:T(8,128)}, u32[]{:S(2)}, u32[]{:S(2)}) async-start(f32[16,256,64]{1,2,0:T(8,128)} %broadcast_in_dim.15), calls=%async_computation.8 | async-start | bytes 2097152 | tf_op jit(solution)/shard_map/all_to_all | solution.py:13
  64.7 81.8 %reduce-scatter.7.cloned.1.call-start = ((), (), s32[]{:S(2)}) async-start(), calls=%async_computation.13 | async-start | bytes 614400 | tf_op jit(solution)/shard_map/reduce_scatter | solution.py:48
  99.9 49.7 %copy-start.10 = (bf16[256,64]{0,1:T(8,128)(2,1)}, bf16[256,64]{0,1:T(8,128)(2,1)S(1)}, u32[]{:S(2)}) copy-start(bf16[256,64]{0,1:T(8,128)(2,1)S(1)} %reduce_sum.37) | copy-start | bytes 98308
  149.6 21.1 %all-to-all-start.1 = ((bf16[16,16,1920]{2,1,0:T(8,128)(2,1)}), bf16[16,16,1920]{2,1,0:T(8,128)(2,1)S(1)}, u32[]{:S(2)}, u32[]{:S(2)}) async-start(bf16[16,16,1920]{2,1,0:T(8,128)(2,1)} %broadcast_in_dim.13), calls=%async_computation.5 | async-start | bytes 1966080 | tf_op jit(solution)/shard_map/all_to_all | solution.py:13
  173.1 30.9 %all-to-all-start.5 = ((bf16[16,16,2,1920]{3,1,2,0:T(8,128)(2,1)}), bf16[16,16,2,1920]{3,1,2,0:T(8,128)(2,1)}, u32[]{:S(2)}, u32[]{:S(2)}) async-start(bf16[16,16,2,1920]{3,1,2,0:T(8,128)(2,1)} %broadcast_in_dim.16), calls=%async_computation.9 | async-start | bytes 3932160 | tf_op jit(solution)/shard_map/all_to_all | solution.py:13
  204.0 15.3 %all-to-all-start.2 = ((f32[8,32,512]{2,1,0:T(8,128)}), f32[8,32,512]{2,1,0:T(8,128)}, u32[]{:S(2)}, u32[]{:S(2)}) async-start(f32[8,32,512]{2,1,0:T(8,128)} %bitcast.110), calls=%async_computation.6 | async-start | bytes 1048576 | tf_op jit(solution)/shard_map/all_to_all | solution.py:67
  208.2 3.0 copy-start.3
  210.0 1.3 copy-start.1
  219.3 15.2 %all-to-all-start.6 = ((f32[8,32,512]{2,1,0:T(8,128)}), f32[8,32,512]{2,1,0:T(8,128)}, u32[]{:S(2)}, u32[]{:S(2)}) async-start(f32[8,32,512]{2,1,0:T(8,128)} %fusion.3), calls=%async_computation.10 | async-start | bytes 1048576 | tf_op jit(solution)/shard_map/all_to_all | solution.py:67
  236.9 4.7 %copy-start.5 = (f32[256,128]{0,1:S(1)}, f32[256,128]{0,1}, u32[]{:S(2)}) copy-start(f32[256,128]{0,1} %copy-done.4) | copy-start | bytes 393220
  236.9 95.6 %all-to-all-start.7 = ((f32[8,1,65536]{2,1,0:T(1,128)}), f32[8,1,65536]{2,1,0:T(1,128)}, u32[]{:S(2)}, u32[]{:S(2)}) async-start(f32[8,1,65536]{2,1,0:T(1,128)} %broadcast_in_dim.17), calls=%async_computation.11 | async-start | bytes 4194304 | tf_op jit(solution)/shard_map/all_to_all | solution.py:13
  241.4 3.2 copy-start.11
  241.4 88.9 %all-reduce.4.cloned.1.call-start = ((), (), s32[]{:S(2)}) async-start(), calls=%async_computation.16 | async-start | bytes 1966080 | tf_op jit(solution)/shard_map/psum | solution.py:169
  332.5 4.9 %copy-start.7 = (bf16[2,512,64]{1,2,0:T(8,128)(2,1)S(1)}, bf16[2,512,64]{1,2,0:T(8,128)(2,1)}, u32[]{:S(2)}) copy-start(bf16[2,512,64]{1,2,0:T(8,128)(2,1)} %param.11) | copy-start | bytes 393220
Sparse Core Ops, SparseCore 0:
  28.2 29.7 reduce-scatter.8
  60.3 36.9 reduce-scatter.4
  99.7 21.1 reduce-scatter.10
  123.2 22.1 reduce-scatter.6
Sparse Core Ops, SparseCore 1:
  43.9 102.6 all-reduce.5
  245.8 84.5 all-reduce.3
where the time goes:
time: 347 us; the launch traced here: 345 us
  waiting for transfers between devices  222 us (64%)
  starting transfers between devices  28.8 us (8%)
  matrix products  23.7 us (7%)
  blocking collectives  21.6 us (6%)
  local copies, waits for them, and re-layouts  21.4 us (6%)
  between operations  16.2 us (5%)
  other arithmetic  12 us (3%)
    psum x1, waiting for transfers between devices, per_device(): lax.psum(upper_partial, MP)  81.9 us
    unnamed x7, waiting for transfers between devices  46.7 us
    reduce_scatter x4, waiting for transfers between devices, sum_in_order(): parts = lax.psum_scatter(parts, axes[k], scatter_dimension=0, tiled=True)  46.6 us
    all_to_all x4, waiting for transfers between devices, sent_to_all(): lax.all_to_all(jnp.broadcast_to(array[None], (length, *array.shape)), axi...  37.1 us
    all_to_all x2, blocking collectives, sent_to_all(): lax.all_to_all(jnp.broadcast_to(array[None], (length, *array.shape)), axi...  21.6 us
    all_to_all x4, starting transfers between devices, sent_to_all(): lax.all_to_all(jnp.broadcast_to(array[None], (length, *array.shape)), axi...  19.3 us
    all_to_all x2, waiting for transfers between devices, sum_at_owner(): lax.all_to_all(parts, axis, split_axis=0, concat_axis=0, tiled=True)  9.43 us
    all_to_all x2, starting transfers between devices, sum_at_owner(): lax.all_to_all(parts, axis, split_axis=0, concat_axis=0, tiled=True)  9.07 us
  transfers between devices with their start and end apart: 12, of which 7 were waited for; matrix products, arithmetic and copies ran while one was open for 10% of the time, Pallas kernels for 0%

commit v1 on v0

--- a/solution.py
+++ b/solution.py
@@ -166,7 +166,9 @@
     pre_back = jnp.stack([gate_back, up_back], axis=1).astype(jnp.bfloat16)
     back_all = gathered_copies(pre_back, MP, 0)
     upper_partial = jnp.einsum("tkr,tkf->krf", low_part, back_all.astype(single_float))
-    gate_up_output_factor_gradient = adapter_scale * scale_factor * lax.psum(upper_partial, MP)
+    gate_up_output_factor_gradient = (
+        adapter_scale * scale_factor * jnp.sum(lax.all_gather(upper_partial, MP), axis=0)
+    )
     back_low_part = jnp.einsum(
         "tkf,krf->tkr", back_all, gate_up_output_factor, preferred_element_type=single_float
     )

time: 347 us -> 306 us (0.88)
  waiting for transfers between devices: 222 us -> 138 us
  blocking collectives: 21.6 us -> 76.5 us
  starting transfers between devices: 28.8 us -> 18.8 us
  local copies, waits for them, and re-layouts: 21.4 us -> 16.7 us
  other arithmetic: 12 us -> 15.6 us
    psum x1 -> x0, waiting for transfers between devices: 81.9 us -> none  [per_device(): lax.psum(upper_partial, MP)]
    all_to_all x2 -> x4, blocking collectives: 21.6 us -> 76.5 us  [sent_to_all(): lax.all_to_all(jnp.broadcast_to(array[None], (length, *array.shape)), axi...]
    all_to_all x4 -> x2, waiting for transfers between devices: 37.1 us -> 23.1 us  [sent_to_all(): lax.all_to_all(jnp.broadcast_to(array[None], (length, *array.shape)), axi...]
    all_gather x0 -> x1, waiting for transfers between devices: none -> 11.8 us  [per_device(): lax.all_gather(upper_partial, MP)]
    all_to_all x4 -> x2, starting transfers between devices: 19.3 us -> 10.1 us  [sent_to_all(): lax.all_to_all(jnp.broadcast_to(array[None], (length, *array.shape)), axi...]
    reduce_sum x0 -> x1, other arithmetic: none -> 6.3 us  [per_device(): jnp.sum(lax.all_gather(upper_partial, MP), axis=0)]
  transfers between devices with their start and end apart: 12 -> 10, of which waited for: 7 -> 7; matrix products, arithmetic and copies ran while one was open for 10% -> 11% of each run, Pallas kernels for 0% -> 0%
where the time goes in v1:
time: 306 us; the launch traced here: 304 us
  waiting for transfers between devices  138 us (45%)
  blocking collectives  76.5 us (25%)
  matrix products  23.1 us (8%)
  starting transfers between devices  18.8 us (6%)
  local copies, waits for them, and re-layouts  16.7 us (5%)
  between operations  16.2 us (5%)
  other arithmetic  15.6 us (5%)
    all_to_all x4, blocking collectives, sent_to_all(): lax.all_to_all(jnp.broadcast_to(array[None], (length, *array.shape)), axi...  76.5 us
    reduce_scatter x4, waiting for transfers between devices, sum_in_order(): parts = lax.psum_scatter(parts, axes[k], scatter_dimension=0, tiled=True)  46.6 us
    unnamed x7, waiting for transfers between devices  45.9 us
    all_to_all x2, waiting for transfers between devices, sent_to_all(): lax.all_to_all(jnp.broadcast_to(array[None], (length, *array.shape)), axi...  23.1 us
    all_gather x1, waiting for transfers between devices, per_device(): lax.all_gather(upper_partial, MP)  11.8 us
    all_to_all x2, starting transfers between devices, sent_to_all(): lax.all_to_all(jnp.broadcast_to(array[None], (length, *array.shape)), axi...  10.1 us
    all_to_all x2, waiting for transfers between devices, sum_at_owner(): lax.all_to_all(parts, axis, split_axis=0, concat_axis=0, tiled=True)  10.1 us
    all_to_all x2, starting transfers between devices, sum_at_owner(): lax.all_to_all(parts, axis, split_axis=0, concat_axis=0, tiled=True)  8.41 us
  transfers between devices with their start and end apart: 10, of which 7 were waited for; matrix products, arithmetic and copies ran while one was open for 11% of the time, Pallas kernels for 0%

profile of v1, /device:TPU:0, one launch (start us, length us, event | category | flops | bytes accessed | tf_op | source)
XLA Modules:
  0.0 304.3 jit_solution(13764649345683172933)
XLA Ops:
  8.0 0.0 reduce-scatter.9.cloned.1.call-start
  8.1 0.9 broadcast_in_dim.12
  9.0 11.7 %all_to_all.41 = bf16[8,32,512]{2,1,0:T(8,128)(2,1)S(1)} all-to-all(bf16[8,32,512]{2,1,0:T(8,128)(2,1)S(1)} %broadcast_in_dim.12), channel_id=1, replica_groups=mesh['dp'=8,'mp_0'=4,'mp_1'=4] {'dp'}, dimensions={0} | all-to-all | bytes 524288 | tf_op jit(solution)/shard_map/all_to_all | solution.py:13
  20.7 1.1 fusion.23
  21.8 3.4 %fusion.22 = f32[256,2,1920]{2,0,1:T(8,128)S(1)} fusion(bf16[256,512,1]{1,0,2:T(8,128)(2,1)S(1)} %bitcast.107, bf16[2,512,1920]{2,1,0:T(8,128)(2,1)} %param.9), kind=kOutput, calls=%fused_computation.40 | convolution fusion | flops 1006632960 | bytes 8126464 | tf_op jit(solution)/shard_map/td,kdf->tkf/dot_general | solution.py:127
  25.2 0.7 bitcast_add_fusion
  25.9 1.6 fusion.19
  27.5 1.4 copy.44
  28.9 0.0 reduce-scatter.9.cloned.1.call-update
  28.9 0.0 reduce-scatter.5.cloned.1.call-start
  29.0 3.0 copy.52
  32.0 0.0 all-reduce.3.cloned.1.call-start
  32.0 0.7 copy-done.9
  32.7 9.9 %all_to_all.42 = bf16[8,32,512]{2,1,0:T(8,128)(2,1)S(1)} all-to-all(bf16[8,32,512]{2,1,0:T(8,128)(2,1)S(1)} %broadcast_in_dim.14), channel_id=1, replica_groups=mesh['dp'=8,'mp_0'=4,'mp_1'=4] {'dp'}, dimensions={0} | all-to-all | bytes 524288 | tf_op jit(solution)/shard_map/all_to_all | solution.py:13
  42.7 2.0 fusion.25
  44.7 0.0 all-reduce.3.cloned.1.call-update
  44.7 0.0 reduce-scatter.11.cloned.1.call-start
  44.7 14.1 %reduce-scatter.9.cloned.1.call-done = f32[4,8,2,1920]{3,1,2,0:T(8,128)} async-done(((f32[16,8,2,1920]{3,1,2,0:T(8,128)}), f32[4,8,2,1920]{3,1,2,0:T(8,128)}) %reduce-scatter.9.cloned.1.call-update) | async-done | bytes 491536 | tf_op jit(solution)/shard_map/reduce_scatter | solution.py:48
  58.8 0.2 fusion.26
  59.1 1.1 broadcast_in_dim.15
  60.1 5.5 %all-to-all-start.4 = ((f32[16,256,64]{1,2,0:T(8,128)}), f32[16,256,64]{1,2,0:T(8,128)}, u32[]{:S(2)}, u32[]{:S(2)}) async-start(f32[16,256,64]{1,2,0:T(8,128)} %broadcast_in_dim.15), calls=%async_computation.8 | async-start | bytes 2097152 | tf_op jit(solution)/shard_map/all_to_all | solution.py:13
  65.6 0.0 reduce-scatter.7.cloned.1.call-start
  65.7 32.6 %reduce-scatter.5.cloned.1.call-done = f32[4,8,2,1920]{3,1,2,0:T(8,128)} async-done(((f32[16,8,2,1920]{3,1,2,0:T(8,128)}), f32[4,8,2,1920]{3,1,2,0:T(8,128)}) %reduce-scatter.5.cloned.1.call-update) | async-done | bytes 491536 | tf_op jit(solution)/shard_map/reduce_scatter | solution.py:48
  98.2 0.0 all-gather.3.cloned.1.call-start
  98.3 0.6 dynamic-slice
  99.6 1.3 reduce_sum.46
  100.9 45.8 %all-reduce.3.cloned.1.call-done = f32[256,1920]{1,0:T(8,128)} async-done(((f32[256,1920]{1,0:T(8,128)}), f32[256,1920]{1,0:T(8,128)}) %all-reduce.3.cloned.1.call-update) | async-done | bytes 1966096
  146.7 1.4 fusion.15
  148.2 0.1 broadcast_in_dim.16
  148.3 31.6 %all_to_all.43 = bf16[16,16,2,1920]{3,1,2,0:T(8,128)(2,1)S(1)} all-to-all(bf16[16,16,2,1920]{3,1,2,0:T(8,128)(2,1)S(1)} %broadcast_in_dim.16), channel_id=1, replica_groups=mesh['dp'=8,'mp_0'=4,'mp_1'=4] {'mp_0','mp_1'}, dimensions={0} | all-to-all | bytes 3932160 | tf_op jit(solution)/shard_map/all_to_all | solution.py:13
  180.0 0.1 copy.45
  180.1 1.3 copy-done.1
  181.4 1.4 fusion.27
  182.7 0.0 all-gather.3.cloned.1.call-update
  182.8 0.1 broadcast_in_dim.13
  182.9 23.2 %all_to_all.44 = bf16[16,16,1920]{2,1,0:T(8,128)(2,1)S(1)} all-to-all(bf16[16,16,1920]{2,1,0:T(8,128)(2,1)S(1)} %broadcast_in_dim.13), channel_id=1, replica_groups=mesh['dp'=8,'mp_0'=4,'mp_1'=4] {'mp_0','mp_1'}, dimensions={0} | all-to-all | bytes 1966080 | tf_op jit(solution)/shard_map/all_to_all | solution.py:13
  206.1 0.4 fusion.24
  206.5 0.2 convolution_bitcast_fusion.1
  206.7 0.7 copy.54
  207.4 0.2 convolution_multiply_fusion.2
  207.6 1.5 convolution_add_fusion
  209.1 4.3 %all-to-all-start.2 = ((f32[8,32,512]{2,1,0:T(8,128)}), f32[8,32,512]{2,1,0:T(8,128)}, u32[]{:S(2)}, u32[]{:S(2)}) async-start(f32[8,32,512]{2,1,0:T(8,128)} %bitcast.112), calls=%async_computation.6 | async-start | bytes 1048576 | tf_op jit(solution)/shard_map/all_to_all | solution.py:67
  213.4 3.0 convolution_bitcast_fusion
  216.4 1.1 copy.46
  217.4 0.8 reshape.119
  218.3 4.7 %fusion.3 = f32[8,32,512]{2,1,0:T(8,128)} fusion(bf16[8,32,1920,2]{2,1,0,3:T(8,128)(2,1)} %bitcast.98, bf16[2,512,1920]{2,1,0:T(8,128)(2,1)} %param.9), kind=kOutput, calls=%fused_computation.6 | convolution fusion | flops 1006632960 | bytes 6422528 | tf_op jit(solution)/shard_map/tkf,kdf->td/dot_general | solution.py:186
  223.0 0.8 all-to-all-done.2
  223.8 4.1 %all-to-all-start.6 = ((f32[8,32,512]{2,1,0:T(8,128)}), f32[8,32,512]{2,1,0:T(8,128)}, u32[]{:S(2)}, u32[]{:S(2)}) async-start(f32[8,32,512]{2,1,0:T(8,128)} %fusion.3), calls=%async_computation.10 | async-start | bytes 1048576 | tf_op jit(solution)/shard_map/all_to_all | solution.py:67
  228.0 1.0 pad_maximum_fusion
  229.0 9.3 %all-to-all-done.6 = f32[8,32,512]{2,1,0:T(8,128)} async-done(((f32[8,32,512]{2,1,0:T(8,128)}), f32[8,32,512]{2,1,0:T(8,128)}, u32[]{:S(2)}, u32[]{:S(2)}) %all-to-all-start.6) | async-done | bytes 524320 | tf_op jit(solution)/shard_map/all_to_all | solution.py:67
  238.3 2.4 broadcast_in_dim.17
  240.7 4.7 %all-to-all-start.7 = ((f32[8,1,65536]{2,1,0:T(1,128)}), f32[8,1,65536]{2,1,0:T(1,128)}, u32[]{:S(2)}, u32[]{:S(2)}) async-start(f32[8,1,65536]{2,1,0:T(1,128)} %broadcast_in_dim.17), calls=%async_computation.11 | async-start | bytes 4194304 | tf_op jit(solution)/shard_map/all_to_all | solution.py:13
  245.4 1.1 convolution_multiply_fusion
  246.4 1.7 reduce_sum.45
  248.2 1.1 reduce_sum.47
  249.3 23.0 %all-to-all-done.7 = f32[8,1,65536]{2,1,0:T(1,128)} async-done(((f32[8,1,65536]{2,1,0:T(1,128)}), f32[8,1,65536]{2,1,0:T(1,128)}, u32[]{:S(2)}, u32[]{:S(2)}) %all-to-all-start.7) | async-done | bytes 2097184 | tf_op jit(solution)/shard_map/all_to_all | solution.py:13
  272.3 3.1 %reduce_sum.48 = f32[65536]{0:T(1024)S(1)} reduce(f32[8,1,65536]{2,1,0:T(1,128)} %all-to-all-done.7, f32[]{:T(128)} %constant.15.clone.1), dimensions={0,1}, to_apply=%region_8.9 | reduce | flops 458752 | bytes 2359300 | tf_op jit(solution)/shard_map/reduce_sum | solution.py:72
  275.5 0.7 mul.128
  276.2 0.1 convert_element_type.32
  276.3 0.8 fusion.9
  277.1 0.9 fusion.6
  278.0 11.8 %all-gather.3.cloned.1.call-done = f32[32,64,1920]{2,1,0:T(8,128)} async-done(((f32[2,64,1920]{2,1,0:T(8,128)}), f32[32,64,1920]{2,1,0:T(8,128)}) %all-gather.3.cloned.1.call-update) | async-done | bytes 15728656 | tf_op jit(solution)/shard_map/all_gather | solution.py:170
  289.9 6.3 %reduce_sum.49 = f32[2,64,1920]{2,1,0:T(8,128)S(1)} reduce(f32[16,2,64,1920]{3,2,1,0:T(8,128)} %bitcast.99, f32[]{:T(128)} %constant.15.clone.1), dimensions={0}, to_apply=%region_9.10 | reduce | flops 3686400 | bytes 16711684 | tf_op jit(solution)/shard_map/reduce_sum | solution.py:170
  296.2 1.0 broadcast_multiply_fusion
  (31 shorter events, 0.2 us)
Async XLA Ops:
  8.0 34.7 %copy-start = (bf16[1920,512]{1,0:T(8,128)(2,1)S(1)}, bf16[1920,512]{1,0:T(8,128)(2,1)}, u32[]{:S(2)}) copy-start(bf16[1920,512]{1,0:T(8,128)(2,1)} %param.10) | copy-start | bytes 5898244
  8.0 50.8 %reduce-scatter.9.cloned.1.call-start = ((), (), s32[]{:S(2)}) async-start(), calls=%async_computation.14 | async-start | bytes 2457600 | tf_op jit(solution)/shard_map/reduce_scatter | solution.py:48
  21.8 3.4 %copy-start.2 = (bf16[2,64,1920]{2,1,0:T(8,128)(2,1)S(1)}, bf16[2,64,1920]{2,1,0:T(8,128)(2,1)}, u32[]{:S(2)}) copy-start(bf16[2,64,1920]{2,1,0:T(8,128)(2,1)} %param.12) | copy-start | bytes 1474564
  28.9 69.3 %reduce-scatter.5.cloned.1.call-start = ((), (), s32[]{:S(2)}) async-start(), calls=%async_computation.12 | async-start | bytes 2457600 | tf_op jit(solution)/shard_map/reduce_scatter | solution.py:48
  32.0 0.8 copy-start.9
  32.0 114.7 %all-reduce.3.cloned.1.call-start = ((), (), s32[]{:S(2)}) async-start(), calls=%async_computation.17 | async-start | bytes 3932160
  44.7 14.2 %copy-start.4 = (bf16[64,512]{1,0:T(8,128)(2,1)S(1)}, bf16[64,512]{1,0:T(8,128)(2,1)}, u32[]{:S(2)}) copy-start(bf16[64,512]{1,0:T(8,128)(2,1)} %param.14) | copy-start | bytes 196612
  44.7 102.0 %reduce-scatter.11.cloned.1.call-start = ((), (), s32[]{:S(2)}) async-start(), calls=%async_computation.15 | async-start | bytes 614400 | tf_op jit(solution)/shard_map/reduce_scatter | solution.py:48
  59.0 39.3 %copy-start.10 = (u32[128]{0:T(128)S(1)}, u32[128]{0:T(128)}, u32[]{:S(2)}) copy-start(u32[128]{0:T(128)} %constant.41) | copy-start | bytes 1540
  60.1 86.6 %copy-start.5 = (bf16[1920,64]{0,1:T(8,128)(2,1)S(1)}, bf16[1920,64]{0,1:T(8,128)(2,1)}, u32[]{:S(2)}) copy-start(bf16[1920,64]{0,1:T(8,128)(2,1)} %param.13) | copy-start | bytes 737284
  60.1 39.4 %all-to-all-start.4 = ((f32[16,256,64]{1,2,0:T(8,128)}), f32[16,256,64]{1,2,0:T(8,128)}, u32[]{:S(2)}, u32[]{:S(2)}) async-start(f32[16,256,64]{1,2,0:T(8,128)} %broadcast_in_dim.15), calls=%async_computation.8 | async-start | bytes 2097152 | tf_op jit(solution)/shard_map/all_to_all | solution.py:13
  65.6 81.1 %reduce-scatter.7.cloned.1.call-start = ((), (), s32[]{:S(2)}) async-start(), calls=%async_computation.13 | async-start | bytes 614400 | tf_op jit(solution)/shard_map/reduce_scatter | solution.py:48
  98.2 191.6 %all-gather.3.cloned.1.call-start = ((), (), s32[]{:S(2)}) async-start(), calls=%async_computation.16 | async-start | bytes 16711680 | tf_op jit(solution)/shard_map/all_gather | solution.py:170
  100.9 47.5 %copy-start.7 = (bf16[256,64]{0,1:T(8,128)(2,1)}, bf16[256,64]{0,1:T(8,128)(2,1)S(1)}, u32[]{:S(2)}) copy-start(bf16[256,64]{0,1:T(8,128)(2,1)S(1)} %reduce_sum.46) | copy-start | bytes 98308
  180.1 1.3 copy-start.1
  182.8 23.3 %copy-start.6 = (bf16[1920,64]{0,1:T(8,128)(2,1)S(1)}, bf16[1920,64]{0,1:T(8,128)(2,1)}, u32[]{:S(2)}) copy-start(bf16[1920,64]{0,1:T(8,128)(2,1)} %param.13) | copy-start | bytes 737284
  209.1 14.7 %all-to-all-start.2 = ((f32[8,32,512]{2,1,0:T(8,128)}), f32[8,32,512]{2,1,0:T(8,128)}, u32[]{:S(2)}, u32[]{:S(2)}) async-start(f32[8,32,512]{2,1,0:T(8,128)} %bitcast.112), calls=%async_computation.6 | async-start | bytes 1048576 | tf_op jit(solution)/shard_map/all_to_all | solution.py:67
  223.8 14.5 %all-to-all-start.6 = ((f32[8,32,512]{2,1,0:T(8,128)}), f32[8,32,512]{2,1,0:T(8,128)}, u32[]{:S(2)}, u32[]{:S(2)}) async-start(f32[8,32,512]{2,1,0:T(8,128)} %fusion.3), calls=%async_computation.10 | async-start | bytes 1048576 | tf_op jit(solution)/shard_map/all_to_all | solution.py:67
  240.7 4.7 %copy-start.8 = (bf16[256,64]{0,1:T(8,128)(2,1)S(1)}, bf16[256,64]{0,1:T(8,128)(2,1)}, u32[]{:S(2)}) copy-start(bf16[256,64]{0,1:T(8,128)(2,1)} %copy-done.7) | copy-start | bytes 98308
  240.7 31.7 %all-to-all-start.7 = ((f32[8,1,65536]{2,1,0:T(1,128)}), f32[8,1,65536]{2,1,0:T(1,128)}, u32[]{:S(2)}, u32[]{:S(2)}) async-start(f32[8,1,65536]{2,1,0:T(1,128)} %broadcast_in_dim.17), calls=%async_computation.11 | async-start | bytes 4194304 | tf_op jit(solution)/shard_map/all_to_all | solution.py:13
  248.2 28.2 %copy-start.3 = (bf16[2,512,64]{1,2,0:T(8,128)(2,1)S(1)}, bf16[2,512,64]{1,2,0:T(8,128)(2,1)}, u32[]{:S(2)}) copy-start(bf16[2,512,64]{1,2,0:T(8,128)(2,1)} %param.11) | copy-start | bytes 393220
Sparse Core Ops, SparseCore 0:
  29.1 29.7 reduce-scatter.8
  61.2 36.9 reduce-scatter.4
  100.6 21.1 reduce-scatter.10
  124.1 22.5 reduce-scatter.6
Sparse Core Ops, SparseCore 1:
  44.8 101.9 all-reduce.2
  182.8 106.9 all-gather.2
